TPU v7x, 32 devices: a whole 2x2x4 slice. The times are simulated.
32 devices in a mesh: row: 4 (over z), col: 8 (over y, x, core).
Axes of the slice: x: 2, y: 2, z: 4, core: 2. Of those that a mesh axis runs over, the one named last changes fastest.
Arguments:
- points: float32 [8, 2048], P(None, ('row', 'col')), may hold values from -15 to 15
- noise_level: float32 [2048], P('row'), may hold values from 0.5 to 2
- right_sides: float32 [64, 2048], P(None, 'row'), may hold values from -6 to 6
Outputs:
- solution: float32 [64, 2048], P(None, 'row')
- residual: float32 [64, 2048], P(None, 'row')
- rel_norms: float32 [64], replicated
All inputs are finite; a program needn't handle non-finite values.
Results may differ from a plain program's by a relative error of at most 0.0008.
Values sent between devices are 32-bit elements; how exact they have to be, the bound alone decides.
A program may use at most 64 MiB of HBM per device.

v0:
```python
import math

import jax
import jax.numpy as jnp
from jax import lax
from jax.sharding import PartitionSpec as P

ITERS = 2


HIGH = lax.Precision.HIGHEST


def from_root(value, axis, root):
    mine = lax.axis_index(axis) == root
    return lax.psum(jnp.where(mine, value, jnp.zeros_like(value)), axis)


def products(first, second):
    return lax.dot_general(first, second, (((1,), (1,)), ((), ())), precision=HIGH)


def solve_sym(matrix, target):
    lower = jnp.linalg.cholesky(0.5 * (matrix + matrix.T))
    return jax.scipy.linalg.cho_solve((lower, True), target)


def gram_sum(single):
    return lax.psum(single, "row")


def triple_sum(first, second, third):
    return lax.psum((first, second, third), "row")


def on_device(points, noise_level, right_sides):
    row_count = lax.axis_size("row")
    col_count = lax.axis_size("col")
    row_index = lax.axis_index("row")
    col_index = lax.axis_index("col")
    pts_dev = points.shape[1]
    row_len = pts_dev * col_count
    col_len = pts_dev * row_count
    col_ratio = col_count // row_count
    all_points = lax.all_gather(points, ("row", "col"), axis=1, tiled=True)
    sq_norms = jnp.sum(all_points * all_points, axis=0)
    row_points = lax.dynamic_slice_in_dim(all_points, row_index * row_len, row_len, 1)
    row_sq = lax.dynamic_slice_in_dim(sq_norms, row_index * row_len, row_len, 0)
    col_points = lax.dynamic_slice_in_dim(all_points, col_index * col_len, col_len, 1)
    col_sq = lax.dynamic_slice_in_dim(sq_norms, col_index * col_len, col_len, 0)
    tile_rows = math.gcd(row_len, 512)
    tile_count = row_len // tile_rows
    rhs_count = right_sides.shape[0]
    residual = right_sides
    solution = jnp.zeros_like(residual)
    direction = residual
    gram = gram_sum(products(residual, residual))
    first = gram
    new_gram = gram
    for iteration in range(ITERS):
        source = lax.dynamic_slice_in_dim(direction, col_index % col_ratio * col_len, col_len, 1)
        col_direction = from_root(source, "row", col_index // col_ratio)

        def one_tile(index, result):
            offset = index * tile_rows
            tile_points = lax.dynamic_slice_in_dim(row_points, offset, tile_rows, 1)
            tile_sq = lax.dynamic_slice_in_dim(row_sq, offset, tile_rows, 0)
            sq_dist = (
                tile_sq[:, None]
                + col_sq[None, :]
                - 2.0 * jnp.dot(tile_points.T, col_points, precision=HIGH)
            )
            kernel = jnp.exp(-0.5 * sq_dist)
            return lax.dynamic_update_slice_in_dim(
                result, products(col_direction, kernel), offset, 1
            )

        image = (
            lax.psum(
                lax.fori_loop(
                    0, tile_count, one_tile, jnp.zeros((rhs_count, row_len), jnp.float32)
                ),
                "col",
            )
            + noise_level[None, :] * direction
        )
        curv, cross, image_gram = triple_sum(
            products(direction, image), products(residual, image), products(image, image)
        )
        step_coef = solve_sym(curv, gram)
        solution = solution + jnp.dot(step_coef.T, direction, precision=HIGH)
        residual = residual - jnp.dot(step_coef.T, image, precision=HIGH)
        cross_coef = jnp.dot(cross, step_coef, precision=HIGH)
        quad = jnp.dot(step_coef.T, jnp.dot(image_gram, step_coef, precision=HIGH), precision=HIGH)
        new_gram = gram - cross_coef - cross_coef.T + quad
        if iteration + 1 < ITERS:
            dir_coef = solve_sym(gram, new_gram)
            direction = residual + jnp.dot(dir_coef.T, direction, precision=HIGH)
        gram = new_gram
    rel_norms = jnp.sqrt(jnp.diagonal(new_gram) / jnp.diagonal(first))
    return (solution, residual, rel_norms)


def solution(mesh):
    placed = (P(None, ("row", "col")), P("row"), P(None, "row"))
    return jax.shard_map(
        on_device,
        mesh=mesh,
        in_specs=placed,
        out_specs=(P(None, "row"), P(None, "row"), P()),
        check_vma=False,
    )
```

profile of v0, /device:TPU:0, one launch (start us, length us, event | category | flops | bytes accessed | tf_op | source)
XLA Modules:
  0.0 288.2 jit_solution(189489273139608216)
XLA Ops:
  7.2 1.5 dynamic-slice_select_fusion.1
  8.8 0.7 copy-done.3
  9.5 43.6 %all-gather = f32[32,64,8]{1,2,0:T(8,128)S(1)} all-gather(f32[1,64,8]{1,2,0:T(8,128)S(1)} %bitcast.102), channel_id=1, replica_groups=mesh['row'=4,'col'=8] {'row','col'}, dimensions={0}, use_global_device_ids=true | all-gather | bytes 67584 | tf_op jit(solution)/shard_map/all_gather | solution.py:45
  53.4 0.7 fusion.2
  54.1 2.1 fusion.31
  56.3 0.8 copy-done
  57.3 48.6 %all-reduce.9.cloned.1.call-done = f32[64,512]{1,0:T(8,128)} async-done(((f32[64,512]{1,0:T(8,128)}), f32[64,512]{1,0:T(8,128)}) %all-reduce.9.cloned.1.call-update) | async-done | bytes 131088 | tf_op jit(solution)/shard_map/psum | solution.py:79
  105.9 1.3 fusion.3
  107.5 20.3 %all-reduce.1 = (f32[64,64]{1,0:T(8,128)S(1)}, f32[64,64]{1,0:T(8,128)S(1)}, f32[64,64]{1,0:T(8,128)S(1)}) all-reduce(f32[64,64]{1,0:T(8,128)S(1)} %fusion.32, f32[64,64]{1,0:T(8,128)S(1)} %convolution_bitcast_fusion, f32[64,64]{1,0:T(8,128)S(1)} %fusion.3), channel_id=1, replica_groups=mesh['row'=4,'col'=8] {'row'}, use_global_device_ids=true, to_apply=%region_6.8 | all-reduce | flops 12288 | bytes 98304 | tf_op jit(solution)/shard_map/psum | solution.py:29
  128.1 5.8 %cholesky.70 = f32[64,64]{1,0:T(8,128)S(1)} custom-call(f32[64,64]{1,0:T(8,128)S(1)} %fusion.20), custom_call_target="Cholesky" | custom-call | tf_op jit(solution)/shard_map/jit(cholesky)/cholesky | solution.py:24
  133.9 0.6 compare_reduce_fusion.1
  134.6 0.7 fusion.8
  135.2 4.9 %custom-call.14 = f32[1,64,64]{1,2,0:T(8,128)S(1)} custom-call(f32[1,64,64]{2,1,0:T(8,128)S(1)} %fusion.8), custom_call_target="InvertDiagBlocksLowerTriangular" | custom-call | tf_op jit(solution)/shard_map/jit(_cho_solve)/triangular_solve | solution.py:25
  140.3 5.8 %cholesky.59 = f32[64,64]{1,0:T(8,128)S(1)} custom-call(f32[64,64]{1,0:T(8,128)S(1)} %fusion.26), custom_call_target="Cholesky" | custom-call | tf_op jit(solution)/shard_map/jit(cholesky)/cholesky | solution.py:24
  146.1 0.6 compare_reduce_fusion.2
  146.8 0.7 fusion.7
  147.4 4.9 %custom-call.13 = f32[1,64,64]{1,2,0:T(8,128)S(1)} custom-call(f32[1,64,64]{2,1,0:T(8,128)S(1)} %fusion.7), custom_call_target="InvertDiagBlocksLowerTriangular" | custom-call | tf_op jit(solution)/shard_map/jit(_cho_solve)/triangular_solve | solution.py:25
  154.5 0.6 dynamic-slice_select_fusion
  155.2 31.1 %all-reduce.11.cloned.1.call-done = f32[64,256]{1,0:T(8,128)} async-done(((f32[64,256]{1,0:T(8,128)}), f32[64,256]{1,0:T(8,128)}) %all-reduce.11.cloned.1.call-update) | async-done | bytes 65552 | tf_op jit(solution)/shard_map/psum | solution.py:16
  186.3 2.1 fusion.36
  188.8 0.8 gather_fusion.1
  189.6 53.4 %all-reduce.13.cloned.1.call-done = f32[64,512]{1,0:T(8,128)} async-done(((f32[64,512]{1,0:T(8,128)}), f32[64,512]{1,0:T(8,128)}) %all-reduce.13.cloned.1.call-update) | async-done | bytes 131088 | tf_op jit(solution)/shard_map/psum | solution.py:79
  243.0 0.9 multiply_add_fusion
  244.7 20.3 %all-reduce = (f32[64,64]{1,0:T(8,128)S(1)}, f32[64,64]{1,0:T(8,128)S(1)}, f32[64,64]{1,0:T(8,128)S(1)}) all-reduce(f32[64,64]{1,0:T(8,128)S(1)} %fusion.37, f32[64,64]{1,0:T(8,128)S(1)} %fusion.40, f32[64,64]{1,0:T(8,128)S(1)} %fusion.38), channel_id=1, replica_groups=mesh['row'=4,'col'=8] {'row'}, use_global_device_ids=true, to_apply=%region_10.13 | all-reduce | flops 12288 | bytes 98304 | tf_op jit(solution)/shard_map/psum | solution.py:33
  265.2 5.8 %cholesky.81 = f32[64,64]{1,0:T(8,128)S(1)} custom-call(f32[64,64]{1,0:T(8,128)S(1)} %fusion.14), custom_call_target="Cholesky" | custom-call | tf_op jit(solution)/shard_map/jit(cholesky)/cholesky | solution.py:24
  271.1 0.6 compare_reduce_fusion
  271.7 0.7 fusion.9
  272.4 4.9 %custom-call.15 = f32[1,64,64]{1,2,0:T(8,128)S(1)} custom-call(f32[1,64,64]{2,1,0:T(8,128)S(1)} %fusion.9), custom_call_target="InvertDiagBlocksLowerTriangular" | custom-call | tf_op jit(solution)/shard_map/jit(_cho_solve)/triangular_solve | solution.py:25
  277.7 1.0 convolution_subtract_fusion
  279.3 0.8 gather_fusion
  280.1 1.0 convolution_add_fusion
  281.1 0.5 divide_sqrt_fusion
  (57 shorter events, 6.0 us)
Async XLA Ops:
  7.2 46.9 %all-reduce.7.cloned.1.call-start = ((), (), s32[]{:S(2)}) async-start(), calls=%async_computation | async-start | bytes 131072 | tf_op jit(solution)/shard_map/psum | solution.py:16
  8.7 97.2 %all-reduce.9.cloned.1.call-start = ((), (), s32[]{:S(2)}) async-start(), calls=%async_computation.1 | async-start | bytes 262144 | tf_op jit(solution)/shard_map/psum | solution.py:79
  8.8 0.7 copy-start.3
  56.2 0.9 copy-start
  56.2 49.7 %copy-start.2 = (f32[512]{0:T(512)S(1)}, f32[512]{0:T(512)}, u32[]{:S(2)}) copy-start(f32[512]{0:T(512)} %param.7) | copy-start | bytes 6148
  56.2 130.1 %all-reduce.11.cloned.1.call-start = ((), (), s32[]{:S(2)}) async-start(), calls=%async_computation.2 | async-start | bytes 131072 | tf_op jit(solution)/shard_map/psum | solution.py:16
  105.9 1.3 copy-start.1
  155.2 87.8 %all-reduce.13.cloned.1.call-start = ((), (), s32[]{:S(2)}) async-start(), calls=%async_computation.3 | async-start | bytes 262144 | tf_op jit(solution)/shard_map/psum | solution.py:79
Sparse Core Ops, SparseCore 0:
  10.9 36.9 all-reduce.6
  56.3 49.5 all-reduce.8
  155.3 30.9 all-reduce.10
  189.8 53.1 all-reduce.12
where the time goes:
time: 289 us; the launch traced here: 288 us
  waiting for transfers between devices  133 us (46%)
  blocking collectives  84.1 us (29%)
  other arithmetic  39.9 us (14%)
  between operations  14.1 us (5%)
  matrix products  12.8 us (4%)
  local copies, waits for them, and re-layouts  4.01 us (1%)
    psum x2, waiting for transfers between devices, on_device(): lax.psum(lax.fori_loop(0, tile_count, one_tile, jnp.zeros((rhs_count, row...  102 us
    all_gather x1, blocking collectives, on_device(): all_points = lax.all_gather(points, ('row', 'col'), axis=1, tiled=True)  43.6 us
    psum x2, waiting for transfers between devices, from_root(): return lax.psum(jnp.where(mine, value, jnp.zeros_like(value)), axis)  31.1 us
    psum x1, blocking collectives, triple_sum(): return lax.psum((first, second, third), 'row')  20.3 us
    psum x1, blocking collectives, gram_sum(): return lax.psum(single, 'row')  20.3 us
    another operation x9, other arithmetic, solve_sym(): lower = jnp.linalg.cholesky(0.5 * (matrix + matrix.T))  19.6 us
    another operation x6, other arithmetic, solve_sym(): return jax.scipy.linalg.cho_solve((lower, True), target)  16.7 us
    dot_general x8, matrix products, products(): lax.dot_general(first, second, (((1,), (1,)), ((), ())), precision=HIGH)  6.83 us
  transfers between devices with their start and end apart: 4, of which 3 were waited for; matrix products, arithmetic and copies ran while one was open for 1% of the time, Pallas kernels for 0%

commit v1 on v0

--- a/solution.py
+++ b/solution.py
@@ -1,14 +1,296 @@
+import functools
 import math
 
 import jax
 import jax.numpy as jnp
 from jax import lax
+from jax.experimental import pallas as pl
+from jax.experimental.pallas import tpu as pltpu
 from jax.sharding import PartitionSpec as P
 
 ITERS = 2
-
-
 HIGH = lax.Precision.HIGHEST
+MESH = pl.DeviceIdType.MESH
+F32 = jnp.float32
+BF16 = jnp.bfloat16
+
+
+def bdot(first, second, dims):
+    return lax.dot_general(first, second, (dims, ((), ())), preferred_element_type=F32)
+
+
+def fdot(first, second, dims):
+    return lax.dot_general(
+        first, second, (dims, ((), ())), precision=HIGH, preferred_element_type=F32
+    )
+
+
+NT = ((1,), (1,))
+TN = ((0,), (0,))
+NN = ((1,), (0,))
+
+
+def split2(value):
+    high = value.astype(BF16)
+    return high, (value - high.astype(F32)).astype(BF16)
+
+
+def split3(value):
+    high = value.astype(BF16)
+    rest = value - high.astype(F32)
+    mid = rest.astype(BF16)
+    return high, mid, (rest - mid.astype(F32)).astype(BF16)
+
+
+def solve_spd(matrix, target):
+    size = matrix.shape[0]
+    matrix = 0.5 * (matrix + matrix.T)
+    both = jnp.concatenate([target, matrix], axis=1)
+    width = both.shape[1]
+    base = target.shape[1]
+    panels = size // 8
+    tiles = [both[8 * t : 8 * t + 8] for t in range(panels)]
+    sublane = lax.broadcasted_iota(jnp.int32, (8, width), 0)
+
+    def lane(tile, j):
+        return jnp.broadcast_to(tile[:, j : j + 1], (8, width))
+
+    def row(tile, s):
+        return jnp.broadcast_to(tile[s : s + 1, :], (8, width))
+
+    for k in range(panels):
+        start = base + 8 * k
+        cols = [lane(tiles[k], start + j) for j in range(8)]
+        others = {
+            t: [lane(tiles[t], start + j) for j in range(8)]
+            for t in range(panels)
+            if t != k
+        }
+        panel = tiles[k]
+        for s in range(8):
+            scale = 1.0 / row(cols[s], s)
+            here = sublane == s
+            factor = cols[s]
+
+            def step(value):
+                pivot = row(value, s) * scale
+                return jnp.where(here, pivot, value - factor * pivot)
+
+            panel = step(panel)
+            for j in range(s + 1, 8):
+                cols[j] = step(cols[j])
+        rows = [row(panel, s) for s in range(8)]
+        tiles[k] = panel
+        for t in others:
+            total = others[t][0] * rows[0]
+            for s in range(1, 8):
+                total = total + others[t][s] * rows[s]
+            tiles[t] = tiles[t] - total
+    return jnp.concatenate(tiles, axis=0)[:, :base]
+
+
+def kernel_body(
+    n_row, n_col,
+    pts_ref, noise_ref, rhs_ref,
+    sol_ref, res_ref, rel_ref,
+    pbuf, rbuf, nbuf, left, right, khi, klo, vst, img, dirs,
+    psem, psend, nsem, nsend, zsem, zsend, csem, csend,
+):
+    z = lax.axis_index("row")
+    c = lax.axis_index("col")
+    dim, piece = pts_ref.shape
+    rhs_count, block = rhs_ref.shape
+    total = block * n_row
+    rows = rhs_count // n_col
+
+    barrier = pltpu.get_barrier_semaphore()
+    for dz in range(1, n_row):
+        pl.semaphore_signal(barrier, inc=1, device_id=(lax.rem(z + dz, n_row), c), device_id_type=MESH)
+    for dc in range(1, n_col):
+        pl.semaphore_signal(barrier, inc=1, device_id=(z, lax.rem(c + dc, n_col)), device_id_type=MESH)
+    pl.semaphore_wait(barrier, n_row + n_col - 2)
+
+    mine = pl.ds(pl.multiple_of(c * rows, rows), rows)
+    copies = []
+
+    def send(src, dst, ssem, rsem, device):
+        copy = pltpu.make_async_remote_copy(
+            src_ref=src, dst_ref=dst, send_sem=ssem, recv_sem=rsem,
+            device_id=device, device_id_type=MESH,
+        )
+        copy.start()
+        copies.append(copy)
+        return copy
+
+    p_z, r_z, n_z = [None], [None], [None]
+    for dz in range(1, n_row):
+        dev = (lax.rem(z + dz, n_row), c)
+        p_z.append(send(pts_ref, pbuf.at[z, c], psend.at[dz, 0], psem.at[dz, 0], dev))
+    for dz in range(1, n_row):
+        dev = (lax.rem(z + dz, n_row), c)
+        r_z.append(send(rhs_ref.at[mine, :], rbuf.at[z, mine, :], zsend.at[dz], zsem.at[dz], dev))
+        n_z.append(send(noise_ref, nbuf.at[z], nsend.at[dz], nsem.at[dz], dev))
+    p_c = {}
+    r_c = {}
+    for dc in range(1, n_col):
+        dev = (z, lax.rem(c + dc, n_col))
+        p_c[0, dc] = send(pts_ref, pbuf.at[z, c], psend.at[0, dc], psem.at[0, dc], dev)
+    pbuf[z, c] = pts_ref[...]
+    rbuf[z] = rhs_ref[...]
+    nbuf[z] = noise_ref[...]
+    for dz in range(1, n_row):
+        src_z = lax.rem(z + n_row - dz, n_row)
+        p_z[dz].wait_recv()
+        for dc in range(1, n_col):
+            dev = (z, lax.rem(c + dc, n_col))
+            p_c[dz, dc] = send(pbuf.at[src_z, c], pbuf.at[src_z, c], psend.at[dz, dc], psem.at[dz, dc], dev)
+    for dz in range(1, n_row):
+        src_z = lax.rem(z + n_row - dz, n_row)
+        r_z[dz].wait_recv()
+        n_z[dz].wait_recv()
+        for dc in range(1, n_col):
+            dev = (z, lax.rem(c + dc, n_col))
+            part = rbuf.at[src_z, mine, :]
+            r_c[dz, dc] = send(part, part, csend.at[dz, dc], csem.at[dz, dc], dev)
+    for dz in range(n_row):
+        for dc in range(1, n_col):
+            p_c[dz, dc].wait_recv()
+
+    pair = 128 // piece
+    for zz in range(n_row):
+        for m in range(n_col // pair):
+            x = jnp.concatenate([pbuf[zz, m * pair + q] for q in range(pair)], axis=1)
+            half = -0.5 * jnp.sum(x * x, axis=0, keepdims=True)
+            one = jnp.ones_like(half)
+            pad = jnp.zeros((16 - dim - 2, pair * piece), F32)
+            lh, lm, ll = split3(jnp.concatenate([x, half, one, pad], axis=0))
+            rh, rm, rl = split3(jnp.concatenate([x, one, half, pad], axis=0))
+            at = pl.ds(zz * block + m * pair * piece, pair * piece)
+            left[:, at] = jnp.concatenate([lh, lh, lm, lh, ll, lm], axis=0)
+            right[:, at] = jnp.concatenate([rh, rm, rh, rl, rh, rm], axis=0)
+
+    tile = 256
+    wide = 512
+
+    def build(t, carry):
+        at = pl.ds(pl.multiple_of(t * tile, tile), tile)
+        lhs = left[:, at]
+        for w in range(total // wide):
+            cols = pl.ds(w * wide, wide)
+            high, low = split2(jnp.exp(bdot(lhs, right[:, cols], TN)))
+            khi[at, cols] = high
+            klo[at, cols] = low
+        return carry
+
+    lax.fori_loop(0, total // tile, build, 0)
+
+    for dz in range(1, n_row):
+        for dc in range(1, n_col):
+            r_c[dz, dc].wait_recv()
+
+    def operate(source):
+        for zz in range(n_row):
+            high, low = split2(source[zz])
+            vst[pl.ds(0, rhs_count), pl.ds(zz * block, block)] = high
+            vst[pl.ds(rhs_count, rhs_count), pl.ds(zz * block, block)] = low
+        for zz in range(n_row):
+            cols = pl.ds(zz * block, block)
+            main = bdot(vst[...], khi[:, cols], NN)
+            minor = bdot(vst[pl.ds(0, rhs_count), :], klo[:, cols], NN)
+            img[zz] = (main[:rhs_count] + (main[rhs_count:] + minor)) + nbuf[zz] * source[zz]
+
+    def products(first, second):
+        out = fdot(first[0], second[0], NT)
+        for zz in range(1, n_row):
+            out = out + fdot(first[zz], second[zz], NT)
+        return out
+
+    gram = products(rbuf, rbuf)
+    operate(rbuf)
+    coef = solve_spd(products(rbuf, img), gram)
+    first_sum = jnp.zeros((8, rhs_count), F32)
+    ones = jnp.ones((8, block), F32)
+    my_sol = fdot(coef, rhs_ref[...], TN)
+    for copy in copies:
+        copy.wait_send()
+    for zz in range(n_row):
+        base = rbuf[zz]
+        first_sum = first_sum + fdot(ones, base * base, NT)
+        dirs[zz] = base
+        rbuf[zz] = base - fdot(coef, img[zz], TN)
+    dcoef = solve_spd(gram, products(rbuf, rbuf))
+    gram = products(rbuf, rbuf)
+    for zz in range(n_row):
+        dirs[zz] = rbuf[zz] + fdot(dcoef, dirs[zz], TN)
+    operate(dirs)
+    coef = solve_spd(products(dirs, img), gram)
+    sol_ref[...] = my_sol + fdot(coef, dirs[z], TN)
+    last_sum = jnp.zeros((8, rhs_count), F32)
+    for zz in range(n_row):
+        new = rbuf[zz] - fdot(coef, img[zz], TN)
+        img[zz] = new
+        last_sum = last_sum + fdot(ones, new * new, NT)
+    res_ref[...] = img[z]
+    rel_ref[...] = jnp.sqrt(last_sum / first_sum)[0:1]
+
+
+def fits(n_row, n_col, points, right_sides):
+    rhs_count, block = right_sides.shape
+    dim, piece = points.shape
+    total = block * n_row
+    return (
+        rhs_count == 64
+        and rhs_count % (8 * n_col) == 0
+        and 128 % piece == 0
+        and n_col % (128 // piece) == 0
+        and total % 512 == 0
+        and block % 128 == 0
+        and dim <= 14
+        and total * total * 4 <= 20 * 2**20
+    )
+
+
+def fused(points, noise_level, right_sides):
+    n_row = lax.axis_size("row")
+    n_col = lax.axis_size("col")
+    rhs_count, block = right_sides.shape
+    dim, piece = points.shape
+    total = block * n_row
+    vmem = pl.BlockSpec(memory_space=pltpu.VMEM)
+    sol, res, rel = pl.pallas_call(
+        functools.partial(kernel_body, n_row, n_col),
+        out_shape=(
+            jax.ShapeDtypeStruct((rhs_count, block), F32),
+            jax.ShapeDtypeStruct((rhs_count, block), F32),
+            jax.ShapeDtypeStruct((1, rhs_count), F32),
+        ),
+        in_specs=[vmem] * 3,
+        out_specs=(vmem,) * 3,
+        scratch_shapes=[
+            pltpu.VMEM((n_row, n_col, dim, piece), F32),
+            pltpu.VMEM((n_row, rhs_count, block), F32),
+            pltpu.VMEM((n_row, 1, block), F32),
+            pltpu.VMEM((96, total), BF16),
+            pltpu.VMEM((96, total), BF16),
+            pltpu.VMEM((total, total), BF16),
+            pltpu.VMEM((total, total), BF16),
+            pltpu.VMEM((2 * rhs_count, total), BF16),
+            pltpu.VMEM((n_row, rhs_count, block), F32),
+            pltpu.VMEM((n_row, rhs_count, block), F32),
+            pltpu.SemaphoreType.DMA((n_row, n_col)),
+            pltpu.SemaphoreType.DMA((n_row, n_col)),
+            pltpu.SemaphoreType.DMA((n_row,)),
+            pltpu.SemaphoreType.DMA((n_row,)),
+            pltpu.SemaphoreType.DMA((n_row,)),
+            pltpu.SemaphoreType.DMA((n_row,)),
+            pltpu.SemaphoreType.DMA((n_row, n_col)),
+            pltpu.SemaphoreType.DMA((n_row, n_col)),
+        ],
+        compiler_params=pltpu.CompilerParams(
+            collective_id=0, has_side_effects=True, vmem_limit_bytes=60 * 2**20
+        ),
+    )(points, noise_level[None, :], right_sides)
+    return sol, res, rel[0]
 
 
 def from_root(value, axis, root):
@@ -36,6 +318,8 @@
 def on_device(points, noise_level, right_sides):
     row_count = lax.axis_size("row")
     col_count = lax.axis_size("col")
+    if fits(row_count, col_count, points, right_sides):
+        return fused(points, noise_level, right_sides)
     row_index = lax.axis_index("row")
     col_index = lax.axis_index("col")
     pts_dev = points.shape[1]

time: 289 us -> 42.2 us (0.15)
  waiting for transfers between devices: 133 us -> 0 us
  blocking collectives: 84.1 us -> 0 us
  other arithmetic: 39.9 us -> 0 us
  Pallas kernels: 0 us -> 38.6 us
  between operations: 14.1 us -> 0.65 us
  matrix products: 12.8 us -> 0 us
    psum x4 -> x0, waiting for transfers between devices: 133 us -> none  [the longest x2 102 us: on_device(): lax.psum(lax.fori_loop(0, tile_count, one_tile, jnp.zeros((rhs_count, row...]
    all_gather x1 -> x0, blocking collectives: 43.6 us -> none  [on_device(): all_points = lax.all_gather(points, ('row', 'col'), axis=1, tiled=True)]
    psum x2 -> x0, blocking collectives: 40.5 us -> none  [the longest x1 20.3 us: triple_sum(): return lax.psum((first, second, third), 'row')]
    pallas_call x0 -> x1, Pallas kernels: none -> 38.6 us  [fused(): pl.pallas_call(functools.partial(kernel_body, n_row, n_col), out_shape=(j...]
    another operation x15 -> x0, other arithmetic: 36.2 us -> none  [the longest x9 19.6 us: solve_sym(): lower = jnp.linalg.cholesky(0.5 * (matrix + matrix.T))]
    dot_general x20 -> x0, matrix products: 11.6 us -> none  [the longest x8 6.83 us: products(): lax.dot_general(first, second, (((1,), (1,)), ((), ())), precision=HIGH)]
  transfers between devices with their start and end apart: 4 -> 0, of which waited for: 3 -> 0; matrix products, arithmetic and copies ran while one was open for 1% -> 0% of each run, Pallas kernels for 0% -> 0%
where the time goes in v1:
time: 42.2 us; the launch traced here: 42.1 us
  Pallas kernels  38.6 us (91%)
  local copies, waits for them, and re-layouts  2.79 us (7%)
  between operations  0.65 us (2%)
    pallas_call x1, Pallas kernels, fused(): pl.pallas_call(functools.partial(kernel_body, n_row, n_col), out_shape=(j...  38.6 us
    unnamed x7, local copies, waits for them, and re-layouts  2.79 us

profile of v1, /device:TPU:0, one launch (start us, length us, event | category | flops | bytes accessed | tf_op | source)
XLA Modules:
  0.0 42.1 jit_solution(1375128189572699977)
XLA Ops:
  0.6 38.6 %shard_map.58 = (f32[64,512]{1,0:T(8,128)}, f32[64,512]{1,0:T(8,128)}, f32[1,64]{1,0:T(1,128)}) custom-call(f32[8,64]{1,0:T(8,128)} %pts_ref.1, f32[1,512]{1,0:T(1,128)} %bitcast.2, f32[64,512]{1,0:T(8,128)} %rhs_ref.1), custom_call_target="tpu_custom_call" | custom-call | tf_op jit(solution)/shard_map/pallas_call | solution.py:260
  39.3 0.0 copy-start
  39.3 1.6 %copy.9 = f32[64,512]{1,0:T(8,128)} copy(f32[64,512]{1,0:T(8,128)} %get-tuple-element.12) | data formatting | bytes 262144
  40.9 0.0 copy-done
  40.9 0.0 copy-start.1
  40.9 0.7 %copy.10 = f32[64,512]{1,0:T(8,128)} copy(f32[64,512]{1,0:T(8,128)S(1)} %copy-done) | data formatting | bytes 262144
  41.5 0.0 copy-done.1
  41.6 0.5 %copy.11 = f32[64]{0:T(128)} copy(f32[64]{0:T(128)S(1)} %bitcast.3) | data formatting | bytes 512
Async XLA Ops:
  39.3 1.6 %copy-start = (f32[64,512]{1,0:T(8,128)S(1)}, f32[64,512]{1,0:T(8,128)}, u32[]{:S(2)}) copy-start(f32[64,512]{1,0:T(8,128)} %get-tuple-element.13) | copy-start | bytes 393220
  40.9 0.7 %copy-start.1 = (f32[1,64]{1,0:T(1,128)S(1)}, f32[1,64]{1,0:T(1,128)}, u32[]{:S(2)}) copy-start(f32[1,64]{1,0:T(1,128)} %get-tuple-element.8) | copy-start | bytes 772

commit v2 on v1

--- a/solution.py
+++ b/solution.py
@@ -42,7 +42,7 @@
     return high, mid, (rest - mid.astype(F32)).astype(BF16)
 
 
-def solve_spd(matrix, target):
+def solve_panels(matrix, target, out):
     size = matrix.shape[0]
     matrix = 0.5 * (matrix + matrix.T)
     both = jnp.concatenate([target, matrix], axis=1)
@@ -86,23 +86,38 @@
             for s in range(1, 8):
                 total = total + others[t][s] * rows[s]
             tiles[t] = tiles[t] - total
-    return jnp.concatenate(tiles, axis=0)[:, :base]
+        if k + 1 < panels:
+            yield
+    out.append(jnp.concatenate(tiles, axis=0)[:, :base])
+    yield
+
+
+def solve_spd(matrix, target):
+    out = []
+    for _ in solve_panels(matrix, target, out):
+        pass
+    return out[0]
 
 
 def kernel_body(
     n_row, n_col,
     pts_ref, noise_ref, rhs_ref,
     sol_ref, res_ref, rel_ref,
-    pbuf, rbuf, nbuf, left, right, khi, klo, vst, img, dirs,
-    psem, psend, nsem, nsend, zsem, zsend, csem, csend,
+    pbuf, rbuf, nbuf, left, right, khi, klo, rs, qs, ss, img, next_res, dirs,
+    pzsem, pzsend, pcsem, pcsend, nsem, nsend, zsem, zsend, csem, csend,
 ):
     z = lax.axis_index("row")
     c = lax.axis_index("col")
     dim, piece = pts_ref.shape
     rhs_count, block = rhs_ref.shape
     total = block * n_row
-    rows = rhs_count // n_col
-
+    half_rows = rhs_count // 2
+    core = lax.rem(c, 2)
+    partner = (z, c + 1 - 2 * core)
+
+    pbuf[c, z] = pts_ref[...]
+    nbuf[z] = noise_ref[...]
+    rbuf[z] = rhs_ref[...]
     barrier = pltpu.get_barrier_semaphore()
     for dz in range(1, n_row):
         pl.semaphore_signal(barrier, inc=1, device_id=(lax.rem(z + dz, n_row), c), device_id_type=MESH)
@@ -110,7 +125,7 @@
         pl.semaphore_signal(barrier, inc=1, device_id=(z, lax.rem(c + dc, n_col)), device_id_type=MESH)
     pl.semaphore_wait(barrier, n_row + n_col - 2)
 
-    mine = pl.ds(pl.multiple_of(c * rows, rows), rows)
+    mine = pl.ds(pl.multiple_of(core * half_rows, half_rows), half_rows)
     copies = []
 
     def send(src, dst, ssem, rsem, device):
@@ -125,41 +140,26 @@
     p_z, r_z, n_z = [None], [None], [None]
     for dz in range(1, n_row):
         dev = (lax.rem(z + dz, n_row), c)
-        p_z.append(send(pts_ref, pbuf.at[z, c], psend.at[dz, 0], psem.at[dz, 0], dev))
+        p_z.append(send(pts_ref, pbuf.at[c, z], pzsend.at[dz], pzsem.at[dz], dev))
     for dz in range(1, n_row):
         dev = (lax.rem(z + dz, n_row), c)
         r_z.append(send(rhs_ref.at[mine, :], rbuf.at[z, mine, :], zsend.at[dz], zsem.at[dz], dev))
+    for dz in range(1, n_row):
+        dev = (lax.rem(z + dz, n_row), c)
         n_z.append(send(noise_ref, nbuf.at[z], nsend.at[dz], nsem.at[dz], dev))
-    p_c = {}
-    r_c = {}
+    for dz in range(1, n_row):
+        p_z[dz].wait_recv()
+    p_c = [None]
     for dc in range(1, n_col):
         dev = (z, lax.rem(c + dc, n_col))
-        p_c[0, dc] = send(pts_ref, pbuf.at[z, c], psend.at[0, dc], psem.at[0, dc], dev)
-    pbuf[z, c] = pts_ref[...]
-    rbuf[z] = rhs_ref[...]
-    nbuf[z] = noise_ref[...]
-    for dz in range(1, n_row):
-        src_z = lax.rem(z + n_row - dz, n_row)
-        p_z[dz].wait_recv()
-        for dc in range(1, n_col):
-            dev = (z, lax.rem(c + dc, n_col))
-            p_c[dz, dc] = send(pbuf.at[src_z, c], pbuf.at[src_z, c], psend.at[dz, dc], psem.at[dz, dc], dev)
-    for dz in range(1, n_row):
-        src_z = lax.rem(z + n_row - dz, n_row)
-        r_z[dz].wait_recv()
-        n_z[dz].wait_recv()
-        for dc in range(1, n_col):
-            dev = (z, lax.rem(c + dc, n_col))
-            part = rbuf.at[src_z, mine, :]
-            r_c[dz, dc] = send(part, part, csend.at[dz, dc], csem.at[dz, dc], dev)
-    for dz in range(n_row):
-        for dc in range(1, n_col):
-            p_c[dz, dc].wait_recv()
+        p_c.append(send(pbuf.at[c], pbuf.at[c], pcsend.at[dc], pcsem.at[dc], dev))
+    for dc in range(1, n_col):
+        p_c[dc].wait_recv()
 
     pair = 128 // piece
     for zz in range(n_row):
         for m in range(n_col // pair):
-            x = jnp.concatenate([pbuf[zz, m * pair + q] for q in range(pair)], axis=1)
+            x = jnp.concatenate([pbuf[m * pair + q, zz] for q in range(pair)], axis=1)
             half = -0.5 * jnp.sum(x * x, axis=0, keepdims=True)
             one = jnp.ones_like(half)
             pad = jnp.zeros((16 - dim - 2, pair * piece), F32)
@@ -182,56 +182,102 @@
             klo[at, cols] = low
         return carry
 
-    lax.fori_loop(0, total // tile, build, 0)
-
-    for dz in range(1, n_row):
-        for dc in range(1, n_col):
-            r_c[dz, dc].wait_recv()
-
-    def operate(source):
-        for zz in range(n_row):
-            high, low = split2(source[zz])
-            vst[pl.ds(0, rhs_count), pl.ds(zz * block, block)] = high
-            vst[pl.ds(rhs_count, rhs_count), pl.ds(zz * block, block)] = low
-        for zz in range(n_row):
-            cols = pl.ds(zz * block, block)
-            main = bdot(vst[...], khi[:, cols], NN)
-            minor = bdot(vst[pl.ds(0, rhs_count), :], klo[:, cols], NN)
-            img[zz] = (main[:rhs_count] + (main[rhs_count:] + minor)) + nbuf[zz] * source[zz]
-
-    def products(first, second):
-        out = fdot(first[0], second[0], NT)
-        for zz in range(1, n_row):
-            out = out + fdot(first[zz], second[zz], NT)
-        return out
-
-    gram = products(rbuf, rbuf)
-    operate(rbuf)
-    coef = solve_spd(products(rbuf, img), gram)
-    first_sum = jnp.zeros((8, rhs_count), F32)
-    ones = jnp.ones((8, block), F32)
-    my_sol = fdot(coef, rhs_ref[...], TN)
+    tiles = total // tile
+    steps = [tiles * (q + 1) // n_row for q in range(n_row)]
+    r_c = [None]
+    done = 0
+    for dz in range(1, n_row):
+        lax.fori_loop(done, steps[dz - 1], build, 0)
+        done = steps[dz - 1]
+        src_z = lax.rem(z + n_row - dz, n_row)
+        r_z[dz].wait_recv()
+        part = rbuf.at[src_z, mine, :]
+        r_c.append(send(part, part, csend.at[dz], csem.at[dz], partner))
+    lax.fori_loop(done, tiles, build, 0)
+    for dz in range(1, n_row):
+        n_z[dz].wait_recv()
+        r_c[dz].wait_recv()
     for copy in copies:
         copy.wait_send()
-    for zz in range(n_row):
-        base = rbuf[zz]
-        first_sum = first_sum + fdot(ones, base * base, NT)
-        dirs[zz] = base
-        rbuf[zz] = base - fdot(coef, img[zz], TN)
-    dcoef = solve_spd(gram, products(rbuf, rbuf))
-    gram = products(rbuf, rbuf)
-    for zz in range(n_row):
-        dirs[zz] = rbuf[zz] + fdot(dcoef, dirs[zz], TN)
-    operate(dirs)
-    coef = solve_spd(products(dirs, img), gram)
-    sol_ref[...] = my_sol + fdot(coef, dirs[z], TN)
-    last_sum = jnp.zeros((8, rhs_count), F32)
-    for zz in range(n_row):
-        new = rbuf[zz] - fdot(coef, img[zz], TN)
-        img[zz] = new
-        last_sum = last_sum + fdot(ones, new * new, NT)
-    res_ref[...] = img[z]
-    rel_ref[...] = jnp.sqrt(last_sum / first_sum)[0:1]
+
+    top = pl.ds(0, rhs_count)
+    low_half = pl.ds(rhs_count, rhs_count)
+
+    def keep(stack, at, value):
+        high, low = split2(value)
+        stack[top, at] = high
+        stack[low_half, at] = low
+
+    def products(first, second):
+        out = bdot(first[...], second[...], NT)
+        upper, lower = out[:rhs_count], out[rhs_count:]
+        both = upper + lower
+        return both[:, :rhs_count] + both[:, rhs_count:]
+
+    def weights(coef):
+        turned = coef.T
+        high, low = split2(jnp.concatenate([turned, turned], axis=1))
+        return jnp.concatenate([high, low], axis=0)
+
+    def apply(stacked, source):
+        out = bdot(stacked, source, NN)
+        return out[:rhs_count] + out[rhs_count:]
+
+    chunk = min(256, block)
+    spots = [
+        (zz, pl.ds(q * chunk, chunk), pl.ds(zz * block + q * chunk, chunk))
+        for zz in range(n_row)
+        for q in range(block // chunk)
+    ]
+
+    def operate(source, stack, beside=None):
+        for zz, inner, cols in spots:
+            main = bdot(stack[...], khi[:, cols], NN)
+            minor = bdot(stack[top, :], klo[:, cols], NN)
+            value = (main[:rhs_count] + (main[rhs_count:] + minor)) + nbuf[zz, :, inner] * source[zz, :, inner]
+            img[zz, :, inner] = value
+            keep(qs, cols, value)
+            if beside is not None:
+                next(beside, None)
+
+    def square_sums(squares):
+        return fdot(jnp.ones((8, squares.shape[1]), F32), squares, NT)
+
+    own = pl.ds(pl.multiple_of(z * block, block), block)
+    first_squares = jnp.zeros((rhs_count, chunk), F32)
+    for zz, inner, cols in spots:
+        base = rbuf[zz, :, inner]
+        keep(rs, cols, base)
+        first_squares = first_squares + base * base
+    gram = products(rs, rs)
+    same = lax.broadcasted_iota(jnp.int32, gram.shape, 0) == lax.broadcasted_iota(jnp.int32, gram.shape, 1)
+    inverse = []
+    beside = solve_panels(gram, same.astype(F32), inverse)
+    operate(rbuf, rs, beside)
+    for _ in beside:
+        pass
+    first_sum = square_sums(first_squares)
+    stacked = weights(solve_spd(products(rs, qs), gram))
+    for zz, inner, cols in spots:
+        value = rbuf[zz, :, inner] - apply(stacked, qs[:, cols])
+        next_res[zz, :, inner] = value
+        keep(ss, cols, value)
+    my_sol = apply(stacked, rs[:, own])
+    gram = products(ss, ss)
+    stacked = weights(fdot(inverse[0], gram, NN))
+    for zz, inner, cols in spots:
+        value = next_res[zz, :, inner] + apply(stacked, rs[:, cols])
+        dirs[zz, :, inner] = value
+        keep(ss, cols, value)
+    operate(dirs, ss)
+    stacked = weights(solve_spd(products(ss, qs), gram))
+    last_squares = jnp.zeros((rhs_count, chunk), F32)
+    for zz, inner, cols in spots:
+        value = next_res[zz, :, inner] - apply(stacked, qs[:, cols])
+        last_squares = last_squares + value * value
+    sol_ref[...] = my_sol + apply(stacked, ss[:, own])
+    res_ref[...] = next_res[z] - apply(stacked, qs[:, own])
+    rel_ref[...] = jnp.sqrt(square_sums(last_squares) / first_sum)[0:1]
 
 
 def fits(n_row, n_col, points, right_sides):
@@ -240,7 +286,7 @@
     total = block * n_row
     return (
         rhs_count == 64
-        and rhs_count % (8 * n_col) == 0
+        and n_col % 2 == 0
         and 128 % piece == 0
         and n_col % (128 // piece) == 0
         and total % 512 == 0
@@ -267,7 +313,7 @@
         in_specs=[vmem] * 3,
         out_specs=(vmem,) * 3,
         scratch_shapes=[
-            pltpu.VMEM((n_row, n_col, dim, piece), F32),
+            pltpu.VMEM((n_col, n_row, dim, piece), F32),
             pltpu.VMEM((n_row, rhs_count, block), F32),
             pltpu.VMEM((n_row, 1, block), F32),
             pltpu.VMEM((96, total), BF16),
@@ -275,16 +321,21 @@
             pltpu.VMEM((total, total), BF16),
             pltpu.VMEM((total, total), BF16),
             pltpu.VMEM((2 * rhs_count, total), BF16),
+            pltpu.VMEM((2 * rhs_count, total), BF16),
+            pltpu.VMEM((2 * rhs_count, total), BF16),
             pltpu.VMEM((n_row, rhs_count, block), F32),
             pltpu.VMEM((n_row, rhs_count, block), F32),
-            pltpu.SemaphoreType.DMA((n_row, n_col)),
-            pltpu.SemaphoreType.DMA((n_row, n_col)),
-            pltpu.SemaphoreType.DMA((n_row,)),
-            pltpu.SemaphoreType.DMA((n_row,)),
-            pltpu.SemaphoreType.DMA((n_row,)),
-            pltpu.SemaphoreType.DMA((n_row,)),
-            pltpu.SemaphoreType.DMA((n_row, n_col)),
-            pltpu.SemaphoreType.DMA((n_row, n_col)),
+            pltpu.VMEM((n_row, rhs_count, block), F32),
+            pltpu.SemaphoreType.DMA((n_row,)),
+            pltpu.SemaphoreType.DMA((n_row,)),
+            pltpu.SemaphoreType.DMA((n_col,)),
+            pltpu.SemaphoreType.DMA((n_col,)),
+            pltpu.SemaphoreType.DMA((n_row,)),
+            pltpu.SemaphoreType.DMA((n_row,)),
+            pltpu.SemaphoreType.DMA((n_row,)),
+            pltpu.SemaphoreType.DMA((n_row,)),
+            pltpu.SemaphoreType.DMA((n_row,)),
+            pltpu.SemaphoreType.DMA((n_row,)),
         ],
         compiler_params=pltpu.CompilerParams(
             collective_id=0, has_side_effects=True, vmem_limit_bytes=60 * 2**20

time: 42.2 us -> 37.7 us (0.89)
  Pallas kernels: 38.6 us -> 34.1 us
    pallas_call x1, Pallas kernels: 38.6 us -> 34.1 us  [fused(): pl.pallas_call(functools.partial(kernel_body, n_row, n_col), out_shape=(j...]
where the time goes in v2:
time: 37.7 us; the launch traced here: 37.6 us
  Pallas kernels  34.1 us (90%)
  local copies, waits for them, and re-layouts  2.79 us (7%)
  between operations  0.65 us (2%)
    pallas_call x1, Pallas kernels, fused(): pl.pallas_call(functools.partial(kernel_body, n_row, n_col), out_shape=(j...  34.1 us
    unnamed x7, local copies, waits for them, and re-layouts  2.79 us

profile of v2, /device:TPU:0, one launch (start us, length us, event | category | flops | bytes accessed | tf_op | source)
XLA Modules:
  0.0 37.6 jit_solution(14245310528550377739)
XLA Ops:
  0.6 34.1 %shard_map.58 = (f32[64,512]{1,0:T(8,128)}, f32[64,512]{1,0:T(8,128)}, f32[1,64]{1,0:T(1,128)}) custom-call(f32[8,64]{1,0:T(8,128)} %pts_ref.1, f32[1,512]{1,0:T(1,128)} %bitcast.2, f32[64,512]{1,0:T(8,128)} %rhs_ref.1), custom_call_target="tpu_custom_call" | custom-call | tf_op jit(solution)/shard_map/pallas_call | solution.py:306
  34.7 0.0 copy-start
  34.8 1.6 %copy.9 = f32[64,512]{1,0:T(8,128)} copy(f32[64,512]{1,0:T(8,128)} %get-tuple-element.12) | data formatting | bytes 262144
  36.4 0.0 copy-done
  36.4 0.0 copy-start.1
  36.4 0.7 %copy.10 = f32[64,512]{1,0:T(8,128)} copy(f32[64,512]{1,0:T(8,128)S(1)} %copy-done) | data formatting | bytes 262144
  37.0 0.0 copy-done.1
  37.0 0.5 %copy.11 = f32[64]{0:T(128)} copy(f32[64]{0:T(128)S(1)} %bitcast.3) | data formatting | bytes 512
Async XLA Ops:
  34.7 1.6 %copy-start = (f32[64,512]{1,0:T(8,128)S(1)}, f32[64,512]{1,0:T(8,128)}, u32[]{:S(2)}) copy-start(f32[64,512]{1,0:T(8,128)} %get-tuple-element.13) | copy-start | bytes 393220
  36.4 0.7 %copy-start.1 = (f32[1,64]{1,0:T(1,128)S(1)}, f32[1,64]{1,0:T(1,128)}, u32[]{:S(2)}) copy-start(f32[1,64]{1,0:T(1,128)} %get-tuple-element.8) | copy-start | bytes 772

commit v3 on v2

--- a/solution.py
+++ b/solution.py
@@ -42,14 +42,14 @@
     return high, mid, (rest - mid.astype(F32)).astype(BF16)
 
 
-def solve_panels(matrix, target, out):
-    size = matrix.shape[0]
+def solve_start(matrix, target):
     matrix = 0.5 * (matrix + matrix.T)
-    both = jnp.concatenate([target, matrix], axis=1)
-    width = both.shape[1]
-    base = target.shape[1]
-    panels = size // 8
-    tiles = [both[8 * t : 8 * t + 8] for t in range(panels)]
+    both = jnp.concatenate([matrix, target], axis=1)
+    return tuple(both[8 * t : 8 * t + 8] for t in range(matrix.shape[0] // 8))
+
+
+def solve_panel(tiles):
+    width = tiles[0].shape[1]
     sublane = lax.broadcasted_iota(jnp.int32, (8, width), 0)
 
     def lane(tile, j):
@@ -58,45 +58,42 @@
     def row(tile, s):
         return jnp.broadcast_to(tile[s : s + 1, :], (8, width))
 
-    for k in range(panels):
-        start = base + 8 * k
-        cols = [lane(tiles[k], start + j) for j in range(8)]
-        others = {
-            t: [lane(tiles[t], start + j) for j in range(8)]
-            for t in range(panels)
-            if t != k
-        }
-        panel = tiles[k]
-        for s in range(8):
-            scale = 1.0 / row(cols[s], s)
-            here = sublane == s
-            factor = cols[s]
-
-            def step(value):
-                pivot = row(value, s) * scale
-                return jnp.where(here, pivot, value - factor * pivot)
-
-            panel = step(panel)
-            for j in range(s + 1, 8):
-                cols[j] = step(cols[j])
-        rows = [row(panel, s) for s in range(8)]
-        tiles[k] = panel
-        for t in others:
-            total = others[t][0] * rows[0]
-            for s in range(1, 8):
-                total = total + others[t][s] * rows[s]
-            tiles[t] = tiles[t] - total
-        if k + 1 < panels:
-            yield
-    out.append(jnp.concatenate(tiles, axis=0)[:, :base])
-    yield
+    def turn(tile):
+        return pltpu.roll(tile, width - 8, 1)
+
+    cols = [lane(tiles[0], j) for j in range(8)]
+    others = [[lane(tile, j) for j in range(8)] for tile in tiles[1:]]
+    panel = turn(tiles[0])
+    rest = [turn(tile) for tile in tiles[1:]]
+    for s in range(8):
+        scale = 1.0 / row(cols[s], s)
+        here = sublane == s
+        factor = cols[s]
+
+        def step(value):
+            pivot = row(value, s) * scale
+            return jnp.where(here, pivot, value - factor * pivot)
+
+        panel = step(panel)
+        for j in range(s + 1, 8):
+            cols[j] = step(cols[j])
+    rows = [row(panel, s) for s in range(8)]
+    out = []
+    for tile, factors in zip(rest, others):
+        total = factors[0] * rows[0]
+        for s in range(1, 8):
+            total = total + factors[s] * rows[s]
+        out.append(tile - total)
+    return tuple(out) + (panel,)
+
+
+def solve_end(tiles):
+    return jnp.concatenate(tiles, axis=0)[:, : 8 * len(tiles)]
 
 
 def solve_spd(matrix, target):
-    out = []
-    for _ in solve_panels(matrix, target, out):
-        pass
-    return out[0]
+    tiles = solve_start(matrix, target)
+    return solve_end(lax.fori_loop(0, len(tiles), lambda _, now: solve_panel(now), tiles))
 
 
 def kernel_body(
@@ -104,7 +101,7 @@
     pts_ref, noise_ref, rhs_ref,
     sol_ref, res_ref, rel_ref,
     pbuf, rbuf, nbuf, left, right, khi, klo, rs, qs, ss, img, next_res, dirs,
-    pzsem, pzsend, pcsem, pcsend, nsem, nsend, zsem, zsend, csem, csend,
+    pzsem, pzsend, pcsem, pcsend, nsem, nsend, zsem, zsend, csem, csend, lsem,
 ):
     z = lax.axis_index("row")
     c = lax.axis_index("col")
@@ -115,15 +112,21 @@
     core = lax.rem(c, 2)
     partner = (z, c + 1 - 2 * core)
 
-    pbuf[c, z] = pts_ref[...]
-    nbuf[z] = noise_ref[...]
-    rbuf[z] = rhs_ref[...]
+    local = [
+        pltpu.make_async_copy(pts_ref, pbuf.at[c, z], lsem.at[0]),
+        pltpu.make_async_copy(rhs_ref, rbuf.at[z], lsem.at[1]),
+        pltpu.make_async_copy(noise_ref, nbuf.at[z], lsem.at[2]),
+    ]
+    for copy in local:
+        copy.start()
     barrier = pltpu.get_barrier_semaphore()
     for dz in range(1, n_row):
         pl.semaphore_signal(barrier, inc=1, device_id=(lax.rem(z + dz, n_row), c), device_id_type=MESH)
     for dc in range(1, n_col):
         pl.semaphore_signal(barrier, inc=1, device_id=(z, lax.rem(c + dc, n_col)), device_id_type=MESH)
     pl.semaphore_wait(barrier, n_row + n_col - 2)
+    for copy in local:
+        copy.wait()
 
     mine = pl.ds(pl.multiple_of(core * half_rows, half_rows), half_rows)
     copies = []
@@ -140,13 +143,13 @@
     p_z, r_z, n_z = [None], [None], [None]
     for dz in range(1, n_row):
         dev = (lax.rem(z + dz, n_row), c)
-        p_z.append(send(pts_ref, pbuf.at[c, z], pzsend.at[dz], pzsem.at[dz], dev))
+        p_z.append(send(pbuf.at[c, z], pbuf.at[c, z], pzsend.at[dz], pzsem.at[dz], dev))
     for dz in range(1, n_row):
         dev = (lax.rem(z + dz, n_row), c)
-        r_z.append(send(rhs_ref.at[mine, :], rbuf.at[z, mine, :], zsend.at[dz], zsem.at[dz], dev))
+        r_z.append(send(rbuf.at[z, mine, :], rbuf.at[z, mine, :], zsend.at[dz], zsem.at[dz], dev))
     for dz in range(1, n_row):
         dev = (lax.rem(z + dz, n_row), c)
-        n_z.append(send(noise_ref, nbuf.at[z], nsend.at[dz], nsem.at[dz], dev))
+        n_z.append(send(nbuf.at[z], nbuf.at[z], nsend.at[dz], nsem.at[dz], dev))
     for dz in range(1, n_row):
         p_z[dz].wait_recv()
     p_c = [None]
@@ -230,15 +233,28 @@
         for q in range(block // chunk)
     ]
 
-    def operate(source, stack, beside=None):
-        for zz, inner, cols in spots:
+    panels = rhs_count // 8
+
+    def operate(source, stack, tiles=()):
+        per = panels // n_row if panels % n_row == 0 else panels
+
+        def one_block(zz, tiles):
+            cols = pl.ds(pl.multiple_of(zz * block, block), block)
             main = bdot(stack[...], khi[:, cols], NN)
             minor = bdot(stack[top, :], klo[:, cols], NN)
-            value = (main[:rhs_count] + (main[rhs_count:] + minor)) + nbuf[zz, :, inner] * source[zz, :, inner]
-            img[zz, :, inner] = value
+            if tiles and per < panels:
+                for _ in range(per):
+                    tiles = solve_panel(tiles)
+            value = (main[:rhs_count] + (main[rhs_count:] + minor)) + nbuf[zz] * source[zz]
+            img[zz] = value
             keep(qs, cols, value)
-            if beside is not None:
-                next(beside, None)
+            return tiles
+
+        tiles = lax.fori_loop(0, n_row, one_block, tiles)
+        if tiles and per == panels:
+            for _ in range(panels):
+                tiles = solve_panel(tiles)
+        return tiles
 
     def square_sums(squares):
         return fdot(jnp.ones((8, squares.shape[1]), F32), squares, NT)
@@ -251,11 +267,7 @@
         first_squares = first_squares + base * base
     gram = products(rs, rs)
     same = lax.broadcasted_iota(jnp.int32, gram.shape, 0) == lax.broadcasted_iota(jnp.int32, gram.shape, 1)
-    inverse = []
-    beside = solve_panels(gram, same.astype(F32), inverse)
-    operate(rbuf, rs, beside)
-    for _ in beside:
-        pass
+    inverse = solve_end(operate(rbuf, rs, solve_start(gram, same.astype(F32))))
     first_sum = square_sums(first_squares)
     stacked = weights(solve_spd(products(rs, qs), gram))
     for zz, inner, cols in spots:
@@ -264,7 +276,7 @@
         keep(ss, cols, value)
     my_sol = apply(stacked, rs[:, own])
     gram = products(ss, ss)
-    stacked = weights(fdot(inverse[0], gram, NN))
+    stacked = weights(fdot(inverse, gram, NN))
     for zz, inner, cols in spots:
         value = next_res[zz, :, inner] + apply(stacked, rs[:, cols])
         dirs[zz, :, inner] = value
@@ -310,7 +322,7 @@
             jax.ShapeDtypeStruct((rhs_count, block), F32),
             jax.ShapeDtypeStruct((1, rhs_count), F32),
         ),
-        in_specs=[vmem] * 3,
+        in_specs=[pl.BlockSpec(memory_space=pl.ANY)] * 3,
         out_specs=(vmem,) * 3,
         scratch_shapes=[
             pltpu.VMEM((n_col, n_row, dim, piece), F32),
@@ -336,6 +348,7 @@
             pltpu.SemaphoreType.DMA((n_row,)),
             pltpu.SemaphoreType.DMA((n_row,)),
             pltpu.SemaphoreType.DMA((n_row,)),
+            pltpu.SemaphoreType.DMA((3,)),
         ],
         compiler_params=pltpu.CompilerParams(
             collective_id=0, has_side_effects=True, vmem_limit_bytes=60 * 2**20

time: 37.7 us -> 36.9 us (0.979)
  Pallas kernels: 34.1 us -> 33.3 us
    pallas_call x1, Pallas kernels: 34.1 us -> 33.3 us  [fused(): pl.pallas_call(functools.partial(kernel_body, n_row, n_col), out_shape=(j...]
where the time goes in v3:
time: 36.9 us; the launch traced here: 36.8 us
  Pallas kernels  33.3 us (90%)
  local copies, waits for them, and re-layouts  2.79 us (8%)
  between operations  0.65 us (2%)
    pallas_call x1, Pallas kernels, fused(): pl.pallas_call(functools.partial(kernel_body, n_row, n_col), out_shape=(j...  33.3 us
    unnamed x7, local copies, waits for them, and re-layouts  2.79 us

profile of v3, /device:TPU:0, one launch (start us, length us, event | category | flops | bytes accessed | tf_op | source)
XLA Modules:
  0.0 36.8 jit_solution(5498492697414726267)
XLA Ops:
  0.6 33.3 %shard_map.58 = (f32[64,512]{1,0:T(8,128)}, f32[64,512]{1,0:T(8,128)}, f32[1,64]{1,0:T(1,128)}) custom-call(f32[8,64]{1,0:T(8,128)} %pts_ref.1, f32[1,512]{1,0:T(1,128)} %bitcast.2, f32[64,512]{1,0:T(8,128)} %rhs_ref.1), custom_call_target="tpu_custom_call" | custom-call | tf_op jit(solution)/shard_map/pallas_call | solution.py:318
  34.0 0.0 copy-start
  34.0 1.6 %copy.9 = f32[64,512]{1,0:T(8,128)} copy(f32[64,512]{1,0:T(8,128)} %get-tuple-element.12) | data formatting | bytes 262144
  35.6 0.0 copy-done
  35.6 0.0 copy-start.1
  35.6 0.7 %copy.10 = f32[64,512]{1,0:T(8,128)} copy(f32[64,512]{1,0:T(8,128)S(1)} %copy-done) | data formatting | bytes 262144
  36.2 0.0 copy-done.1
  36.3 0.5 %copy.11 = f32[64]{0:T(128)} copy(f32[64]{0:T(128)S(1)} %bitcast.3) | data formatting | bytes 512
Async XLA Ops:
  34.0 1.6 %copy-start = (f32[64,512]{1,0:T(8,128)S(1)}, f32[64,512]{1,0:T(8,128)}, u32[]{:S(2)}) copy-start(f32[64,512]{1,0:T(8,128)} %get-tuple-element.13) | copy-start | bytes 393220
  35.6 0.7 %copy-start.1 = (f32[1,64]{1,0:T(1,128)S(1)}, f32[1,64]{1,0:T(1,128)}, u32[]{:S(2)}) copy-start(f32[1,64]{1,0:T(1,128)} %get-tuple-element.8) | copy-start | bytes 772

commit v4 on v3

--- a/solution.py
+++ b/solution.py
@@ -150,14 +150,16 @@
     for dz in range(1, n_row):
         dev = (lax.rem(z + dz, n_row), c)
         n_z.append(send(nbuf.at[z], nbuf.at[z], nsend.at[dz], nsem.at[dz], dev))
-    for dz in range(1, n_row):
-        p_z[dz].wait_recv()
-    p_c = [None]
-    for dc in range(1, n_col):
-        dev = (z, lax.rem(c + dc, n_col))
-        p_c.append(send(pbuf.at[c], pbuf.at[c], pcsend.at[dc], pcsem.at[dc], dev))
-    for dc in range(1, n_col):
-        p_c[dc].wait_recv()
+    p_c = []
+    for dz in range(n_row):
+        if dz > 0:
+            p_z[dz].wait_recv()
+        from_z = lax.rem(z + n_row - dz, n_row)
+        for dc in range(1, n_col):
+            dev = (z, lax.rem(c + dc, n_col))
+            p_c.append(send(pbuf.at[c, from_z], pbuf.at[c, from_z], pcsend.at[dz, dc], pcsem.at[dz, dc], dev))
+    for copy in p_c:
+        copy.wait_recv()
 
     pair = 128 // piece
     for zz in range(n_row):
@@ -340,8 +342,8 @@
             pltpu.VMEM((n_row, rhs_count, block), F32),
             pltpu.SemaphoreType.DMA((n_row,)),
             pltpu.SemaphoreType.DMA((n_row,)),
-            pltpu.SemaphoreType.DMA((n_col,)),
-            pltpu.SemaphoreType.DMA((n_col,)),
+            pltpu.SemaphoreType.DMA((n_row, n_col)),
+            pltpu.SemaphoreType.DMA((n_row, n_col)),
             pltpu.SemaphoreType.DMA((n_row,)),
             pltpu.SemaphoreType.DMA((n_row,)),
             pltpu.SemaphoreType.DMA((n_row,)),

time: 36.9 us -> 37.4 us (1.014)
  Pallas kernels: 33.3 us -> 33.8 us
    pallas_call x1, Pallas kernels: 33.3 us -> 33.8 us  [fused(): pl.pallas_call(functools.partial(kernel_body, n_row, n_col), out_shape=(j...]
where the time goes in v4:
time: 37.4 us; the launch traced here: 37.3 us
  Pallas kernels  33.8 us (90%)
  local copies, waits for them, and re-layouts  2.79 us (7%)
  between operations  0.65 us (2%)
    pallas_call x1, Pallas kernels, fused(): pl.pallas_call(functools.partial(kernel_body, n_row, n_col), out_shape=(j...  33.8 us
    unnamed x7, local copies, waits for them, and re-layouts  2.79 us

profile of v4, /device:TPU:0, one launch (start us, length us, event | category | flops | bytes accessed | tf_op | source)
XLA Modules:
  0.0 37.3 jit_solution(2710386165081079437)
XLA Ops:
  0.6 33.8 %shard_map.58 = (f32[64,512]{1,0:T(8,128)}, f32[64,512]{1,0:T(8,128)}, f32[1,64]{1,0:T(1,128)}) custom-call(f32[8,64]{1,0:T(8,128)} %pts_ref.1, f32[1,512]{1,0:T(1,128)} %bitcast.2, f32[64,512]{1,0:T(8,128)} %rhs_ref.1), custom_call_target="tpu_custom_call" | custom-call | tf_op jit(solution)/shard_map/pallas_call | solution.py:320
  34.5 0.0 copy-start
  34.5 1.6 %copy.9 = f32[64,512]{1,0:T(8,128)} copy(f32[64,512]{1,0:T(8,128)} %get-tuple-element.12) | data formatting | bytes 262144
  36.1 0.0 copy-done
  36.1 0.0 copy-start.1
  36.1 0.7 %copy.10 = f32[64,512]{1,0:T(8,128)} copy(f32[64,512]{1,0:T(8,128)S(1)} %copy-done) | data formatting | bytes 262144
  36.7 0.0 copy-done.1
  36.8 0.5 %copy.11 = f32[64]{0:T(128)} copy(f32[64]{0:T(128)S(1)} %bitcast.3) | data formatting | bytes 512
Async XLA Ops:
  34.5 1.6 %copy-start = (f32[64,512]{1,0:T(8,128)S(1)}, f32[64,512]{1,0:T(8,128)}, u32[]{:S(2)}) copy-start(f32[64,512]{1,0:T(8,128)} %get-tuple-element.13) | copy-start | bytes 393220
  36.1 0.7 %copy-start.1 = (f32[1,64]{1,0:T(1,128)S(1)}, f32[1,64]{1,0:T(1,128)}, u32[]{:S(2)}) copy-start(f32[1,64]{1,0:T(1,128)} %get-tuple-element.8) | copy-start | bytes 772
